TPU v7x, 512 devices: a 8x2x16 block of a 8x8x16 slice. The times are simulated.
512 devices in a mesh: groups: 2 (over y), seq: 16 (over z), tensor: 8 (over x), sub: 2 (over core).
Axes of the slice: x: 8, y: 2, z: 16, core: 2. Of those that a mesh axis runs over, the one named last changes fastest.
The devices are a block of a 8x8x16 slice.
Arguments:
- image_tokens: bfloat16 [8192, 3072], P(('groups', 'seq')), parts along dimension 0, may hold values from -6 to 6
- text_tokens: bfloat16 [1024, 3072], P(('groups', 'seq')), parts along dimension 0, may hold values from -6 to 6
- timestep: int32 [2], P('groups'), parts along dimension 0, may hold values from 0 to 49
- text_length: int32 [2], P('groups'), parts along dimension 0, may hold values from 128 to 512
- time_table: bfloat16 [50, 3072], replicated, may hold values from -6 to 6
- mod_weight: bfloat16 [3072, 18432], P('seq', ('tensor', 'sub')), may hold values from -0.109375 to 0.109375
- qkv_image: bfloat16 [3072, 6144], P('seq', ('tensor', 'sub')), as said below
- qkv_text: bfloat16 [3072, 6144], P('seq', ('tensor', 'sub')), as said below
- norm_gain: float32 [2, 2, 16, 128], P(None, None, ('tensor', 'sub')), may hold values from 1 to 6
- proj_image: bfloat16 [2048, 3072], P(('tensor', 'sub'), 'seq'), may hold values from -0.125 to 0.125
- proj_text: bfloat16 [2048, 3072], P(('tensor', 'sub'), 'seq'), may hold values from -0.125 to 0.125
Outputs:
- image_out: bfloat16 [8192, 3072], P(('groups', 'seq'), ('tensor', 'sub')), parts along dimension 0
- text_out: bfloat16 [1024, 3072], P(('groups', 'seq'), ('tensor', 'sub')), parts along dimension 0
There are 2 independent parts, one for each index of `groups`. A program takes and returns all parts, laid end to end along the dimension named above; an argument that names none is the same for every part. Nothing has to cross between parts.
Inputs may be any that keep to these rules, and one draw needn't show every extreme that they name: `qkv_image`: entries of standard deviation about 1/sqrt(3072). `qkv_text`: entries of standard deviation about 1/sqrt(3072).
All inputs are finite; a program needn't handle non-finite values.
Results may differ from a plain program's by a relative error of at most 0.0085.
Values may be sent and summed in bfloat16 or wider, within the bound.
A program may use at most 64 MiB of HBM per device.

v0:
```python
import jax
import jax.numpy as jnp
from jax import lax
from jax.sharding import PartitionSpec as P

EPSILON = 1e-06


def copy_for_each(x, axis):
    copies = jnp.broadcast_to(x, (lax.axis_size(axis), *x.shape))
    return lax.all_to_all(copies, axis, split_axis=0, concat_axis=0, tiled=True)


def over_copies(x, axis):
    everything = copy_for_each(x, axis)
    return jnp.sum(everything, axis=0)


def side_by_side(arrays, axis, dim, along):
    ends, at = ([], 0)
    for a in arrays[:-1]:
        at += a.shape[along]
        ends.append(at)
    both = jnp.concatenate(arrays, axis=along)
    return tuple(jnp.split(lax.all_gather(both, axis, axis=dim, tiled=True), ends, axis=along))


def joined_along(tiles, dim):
    shape = list(tiles.shape[1:])
    shape[dim] *= tiles.shape[0]
    return jnp.moveaxis(tiles, 0, dim).reshape(shape)


def gather_directly(x, axis, dim):
    return joined_along(copy_for_each(x, axis), dim)


def modulate(tokens, shift, scaling):
    values = tokens.astype(jnp.float32)
    center = jnp.mean(values, axis=-1, keepdims=True)
    spread = jnp.mean(jnp.square(values - center), axis=-1, keepdims=True)
    normed = (values - center) * lax.rsqrt(spread + EPSILON)
    return (normed * (1.0 + scaling) + shift).astype(jnp.bfloat16)


def head_norm(values, gain):
    return values * lax.rsqrt(jnp.mean(values * values, axis=-1, keepdims=True) + EPSILON) * gain


def split_heads(projected, gains):
    shaped = projected.reshape(projected.shape[0], -1, 3, gains.shape[-1])
    queries = head_norm(shaped[:, :, 0], gains[0]).astype(jnp.bfloat16)
    keys = head_norm(shaped[:, :, 1], gains[1]).astype(jnp.bfloat16)
    values = shaped[:, :, 2].astype(jnp.bfloat16)
    return (queries, keys, values)


def add_rows(source, shards):
    return jnp.dot(source, shards, preferred_element_type=jnp.float32)


def body(
    image_tokens,
    text_tokens,
    timestep,
    text_length,
    time_table,
    mod_weight,
    qkv_image,
    qkv_text,
    norm_gain,
    proj_image,
    proj_text,
):
    columns_all = image_tokens.shape[1]
    embedded = lax.dynamic_index_in_dim(time_table, timestep[0], 0, keepdims=False).astype(
        jnp.float32
    )
    vector = jax.nn.silu(embedded).astype(jnp.bfloat16)
    slab_rows = mod_weight.shape[0]
    vector_rows = lax.dynamic_slice_in_dim(vector, lax.axis_index("seq") * slab_rows, slab_rows)
    partial_value = jnp.dot(vector_rows[None, :], mod_weight, preferred_element_type=jnp.float32)[0]
    summed_rows = over_copies(partial_value, "seq")
    modulation = lax.all_gather(summed_rows, ("tensor", "sub"), axis=0, tiled=True)
    modulation = modulation.reshape(2, 3, columns_all)
    hidden_image = modulate(image_tokens, modulation[0, 0], modulation[0, 1])
    hidden_text = modulate(text_tokens, modulation[1, 0], modulation[1, 1])
    image_count = image_tokens.shape[0]
    text_count = text_tokens.shape[0]
    local_rows = image_count + text_count
    shards = side_by_side((qkv_image, qkv_text), "seq", 0, 1)
    projected_image = add_rows(hidden_image, shards[0])
    projected_text = add_rows(hidden_text, shards[1])
    image_q, image_k, image_v = split_heads(projected_image, norm_gain[0])
    text_q, text_k, text_v = split_heads(projected_text, norm_gain[1])
    heads_here = image_q.shape[1]
    head_size = image_q.shape[2]
    queries = jnp.concatenate([text_q, image_q], axis=0)
    keys = jnp.concatenate([text_k, image_k], axis=0)
    values = jnp.concatenate([text_v, image_v], axis=0)
    keys_values = jnp.stack([keys, values], axis=2).reshape(local_rows, heads_here * 2 * head_size)
    factor = float(head_size) ** (-0.5)
    shards = lax.all_gather(keys_values, "seq", axis=0, tiled=True)
    count = shards.shape[0]
    blocks = shards.reshape(count, heads_here, 2, head_size)
    position = jnp.arange(count, dtype=jnp.int32)
    within = position % local_rows
    owner = position // local_rows
    usable = (within >= text_count) | (owner * text_count + within < text_length[0])
    scores = (
        jnp.einsum("qhd,khd->hqk", queries, blocks[:, :, 0], preferred_element_type=jnp.float32)
        * factor
    )
    scores = jnp.where(usable[None, None, :], scores, -1e30)
    run_max = jnp.full((heads_here, local_rows), -1e30, jnp.float32)
    new_max = jnp.maximum(run_max, jnp.max(scores, axis=-1))
    probs = jnp.exp(scores - new_max[:, :, None])
    run_sum = jnp.sum(probs, axis=-1)
    totals = jnp.einsum(
        "hqk,khd->hqd",
        probs.astype(jnp.bfloat16),
        blocks[:, :, 1],
        preferred_element_type=jnp.float32,
    )
    final_max, run_sum, totals = (new_max, run_sum, totals)
    attended = (
        (totals / run_sum[:, :, None])
        .astype(jnp.bfloat16)
        .transpose(1, 0, 2)
        .reshape(local_rows, heads_here * head_size)
    )
    stacked = jnp.stack([proj_image, proj_text], axis=0)
    width_here = columns_all // lax.axis_size(("tensor", "sub"))
    first = lax.axis_index(("tensor", "sub")) * width_here
    attended_all = lax.all_gather(attended, ("tensor", "sub"), axis=1, tiled=True)
    full_columns = gather_directly(stacked, "seq", 2)
    all_rows = lax.all_to_all(
        full_columns, ("tensor", "sub"), split_axis=2, concat_axis=1, tiled=True
    )
    text_part = jnp.dot(attended_all[:text_count], all_rows[1], preferred_element_type=jnp.float32)
    image_part = jnp.dot(attended_all[text_count:], all_rows[0], preferred_element_type=jnp.float32)
    summed = jnp.concatenate([text_part, image_part], axis=0)
    gates = lax.dynamic_slice_in_dim(modulation[:, 2], first, width_here, 1)
    image_base = lax.dynamic_slice_in_dim(image_tokens, first, width_here, 1).astype(jnp.float32)
    text_base = lax.dynamic_slice_in_dim(text_tokens, first, width_here, 1).astype(jnp.float32)
    image_out = (image_base + gates[0] * summed[text_count:]).astype(jnp.bfloat16)
    text_out = (text_base + gates[1] * summed[:text_count]).astype(jnp.bfloat16)
    return (image_out, text_out)


def solution(mesh):
    return jax.shard_map(
        body,
        mesh=mesh,
        in_specs=(
            P(("groups", "seq"), None),
            P(("groups", "seq"), None),
            P("groups"),
            P("groups"),
            P(),
            P("seq", ("tensor", "sub")),
            P("seq", ("tensor", "sub")),
            P("seq", ("tensor", "sub")),
            P(None, None, ("tensor", "sub"), None),
            P(("tensor", "sub"), "seq"),
            P(("tensor", "sub"), "seq"),
        ),
        out_specs=(
            P(("groups", "seq"), ("tensor", "sub")),
            P(("groups", "seq"), ("tensor", "sub")),
        ),
        check_vma=False,
    )
```

profile of v0, /device:TPU:65, one launch (start us, length us, event | category | flops | bytes accessed | tf_op | source)
XLA Modules:
  0.0 331.8 jit_solution(2012975773529519492)
XLA Ops:
  7.3 1.8 pad_maximum_fusion
  11.6 44.2 %all-to-all-start = ((f32[16,1,1152]{2,1,0:T(1,128)}), f32[16,1,1152]{2,1,0:T(1,128)S(1)}, u32[]{:S(2)}, u32[]{:S(2)}) async-start(f32[16,1,1152]{2,1,0:T(1,128)} %broadcast_in_dim.14), calls=%async_computation | async-start | bytes 147456 | tf_op jit(solution)/shard_map/all_to_all | solution.py:11
  55.9 1.1 convert_reduce_fusion.1
  56.9 1.2 fusion.38
  59.1 8.3 %all-to-all-done = f32[16,1,1152]{2,1,0:T(1,128)S(1)} async-done(((f32[16,1,1152]{2,1,0:T(1,128)}), f32[16,1,1152]{2,1,0:T(1,128)S(1)}, u32[]{:S(2)}, u32[]{:S(2)}) %all-to-all-start) | async-done | bytes 73760 | tf_op jit(solution)/shard_map/all_to_all | solution.py:11
  67.4 1.5 broadcast_in_dim.22
  68.9 4.8 %all-to-all-start.1 = ((bf16[16,2,128,192]{2,3,1,0:T(8,128)(2,1)}), bf16[16,2,128,192]{2,3,1,0:T(8,128)(2,1)}, u32[]{:S(2)}, u32[]{:S(2)}) async-start(bf16[16,2,128,192]{2,3,1,0:T(8,128)(2,1)} %broadcast_in_dim.22), calls=%async_computation.1 | async-start | bytes 3145728 | tf_op jit(solution)/shard_map/all_to_all | solution.py:11
  73.8 20.3 %all-gather = f32[16,1,1152]{2,1,0:T(1,128)S(1)} all-gather(f32[1,1,1152]{2,1,0:T(1,128)S(1)} %reshape.562), channel_id=1, replica_groups=mesh['groups'=2,'seq'=16,'tensor'=8,'sub'=2] {'tensor','sub'}, dimensions={0}, use_global_device_ids=true | all-gather | bytes 78336 | tf_op jit(solution)/shard_map/all_gather | solution.py:84
  94.4 90.3 %all-gather.5.cloned.1.call-done = bf16[3072,768]{1,0:T(8,128)(2,1)} async-done(((bf16[192,768]{1,0:T(8,128)(2,1)}), bf16[3072,768]{1,0:T(8,128)(2,1)}) %all-gather.5.cloned.1.call-update) | async-done | bytes 4718608 | tf_op jit(solution)/shard_map/all_gather | solution.py:25
  184.7 2.2 fusion.14
  187.4 3.0 fusion.12
  192.3 1.5 copy.69
  193.9 13.8 %copy.70 = bf16[2,128,3072]{1,0,2:T(2,128)(2,1)} copy(bf16[2,128,3072]{1,2,0:T(8,128)(2,1)S(1)} %bitcast.86) | data formatting | bytes 3145728 | tf_op jit(solution)/shard_map/reshape | solution.py:31
  207.7 13.5 %all-to-all-start.2 = ((bf16[2,128,3072]{1,0,2:T(2,128)(2,1)}), bf16[2,128,3072]{1,0,2:T(2,128)(2,1)}, u32[]{:S(2)}, u32[]{:S(2)}) async-start(bf16[2,128,3072]{1,0,2:T(2,128)(2,1)} %copy.70), calls=%async_computation.2 | async-start | bytes 3145728 | tf_op jit(solution)/shard_map/all_to_all | solution.py:137
  221.7 38.3 %all-gather.7.cloned.1.call-done = bf16[4608,256]{1,0:T(8,128)(2,1)} async-done(((bf16[288,256]{1,0:T(8,128)(2,1)}), bf16[4608,256]{1,0:T(8,128)(2,1)}) %all-gather.7.cloned.1.call-update) | async-done | bytes 2359312 | tf_op jit(solution)/shard_map/all_gather | solution.py:103
  260.0 4.6 %reshape.557 = bf16[4608,1,2,128]{3,2,0,1:T(2,128)(2,1)S(1)} reshape(bf16[4608,256]{1,0:T(8,128)(2,1)} %all-gather.7.cloned.1.call-done) | data formatting | bytes 4718592 | tf_op jit(solution)/shard_map/reshape | solution.py:105
  264.7 3.4 %fusion.63 = (bf16[4608,1,1,128]{3,2,0,1:T(2,128)(2,1)S(1)}, bf16[4608,1,1,128]{3,2,0,1:T(2,128)(2,1)S(1)}) fusion(bf16[4608,1,2,128]{3,2,0,1:T(2,128)(2,1)S(1)} %reshape.557), kind=kLoop, calls=%fused_computation.110 | loop fusion | bytes 4718592 | tf_op jit(solution)/shard_map/slice | solution.py:111
  268.1 1.3 fusion.66
  270.2 1.6 fusion.28
  271.8 1.0 constant_dynamic-slice_fusion.2
  273.1 1.6 copy.71
  275.9 45.1 %all-gather.9.cloned.1.call-done = bf16[288,2048]{1,0:T(8,128)(2,1)} async-done(((bf16[288,128]{1,0:T(8,128)(2,1)}), bf16[288,2048]{1,0:T(8,128)(2,1)}) %all-gather.9.cloned.1.call-update) | async-done | bytes 1179664 | tf_op jit(solution)/shard_map/all_gather | solution.py:135
  321.0 1.9 fusion.24
  322.9 2.4 fusion.22
  (67 shorter events, 7.8 us)
Async XLA Ops:
  7.2 3.6 %copy-start = (bf16[192,1152]{1,0:T(8,128)(2,1)S(1)}, bf16[192,1152]{1,0:T(8,128)(2,1)}, u32[]{:S(2)}) copy-start(bf16[192,1152]{1,0:T(8,128)(2,1)} %param.16) | copy-start | bytes 1327108
  7.2 50.9 %copy-start.1 = (bf16[256,3072]{1,0:T(8,128)(2,1)S(1)}, bf16[256,3072]{1,0:T(8,128)(2,1)}, u32[]{:S(2)}) copy-start(bf16[256,3072]{1,0:T(8,128)(2,1)} %param.11) | copy-start | bytes 4718596
  7.2 177.5 %all-gather.5.cloned.1.call-start = ((), (), s32[]{:S(2)}) async-start(), calls=%async_computation.3 | async-start | bytes 5013504 | tf_op jit(solution)/shard_map/all_gather | solution.py:25
  9.1 49.9 %copy-start.3 = (bf16[128,192]{0,1:T(8,128)(2,1)S(1)}, bf16[128,192]{0,1:T(8,128)(2,1)}, u32[]{:S(2)}) copy-start(bf16[128,192]{0,1:T(8,128)(2,1)} %param.21) | copy-start | bytes 147460
  9.1 49.9 %copy-start.4 = (bf16[128,192]{0,1:T(8,128)(2,1)S(1)}, bf16[128,192]{0,1:T(8,128)(2,1)}, u32[]{:S(2)}) copy-start(bf16[128,192]{0,1:T(8,128)(2,1)} %param.20) | copy-start | bytes 147460
  9.1 49.9 %copy-start.5 = (f32[2,2,1,128]{3,2,1,0:T(1,128)S(1)}, f32[2,2,1,128]{3,2,1,0:T(1,128)}, u32[]{:S(2)}) copy-start(f32[2,2,1,128]{3,2,1,0:T(1,128)} %param.19) | copy-start | bytes 6148
  11.6 55.7 %all-to-all-start = ((f32[16,1,1152]{2,1,0:T(1,128)}), f32[16,1,1152]{2,1,0:T(1,128)S(1)}, u32[]{:S(2)}, u32[]{:S(2)}) async-start(f32[16,1,1152]{2,1,0:T(1,128)} %broadcast_in_dim.14), calls=%async_computation | async-start | bytes 147456 | tf_op jit(solution)/shard_map/all_to_all | solution.py:11
  59.0 125.6 %copy-start.2 = (bf16[32,3072]{1,0:T(8,128)(2,1)S(1)}, bf16[32,3072]{1,0:T(8,128)(2,1)}, u32[]{:S(2)}) copy-start(bf16[32,3072]{1,0:T(8,128)(2,1)} %param.12) | copy-start | bytes 589828
  68.9 123.5 %all-to-all-start.1 = ((bf16[16,2,128,192]{2,3,1,0:T(8,128)(2,1)}), bf16[16,2,128,192]{2,3,1,0:T(8,128)(2,1)}, u32[]{:S(2)}, u32[]{:S(2)}) async-start(bf16[16,2,128,192]{2,3,1,0:T(8,128)(2,1)} %broadcast_in_dim.22), calls=%async_computation.1 | async-start | bytes 3145728 | tf_op jit(solution)/shard_map/all_to_all | solution.py:11
  73.7 186.4 %all-gather.7.cloned.1.call-start = ((), (), s32[]{:S(2)}) async-start(), calls=%async_computation.4 | async-start | bytes 2506752 | tf_op jit(solution)/shard_map/all_gather | solution.py:103
  207.7 65.4 %all-to-all-start.2 = ((bf16[2,128,3072]{1,0,2:T(2,128)(2,1)}), bf16[2,128,3072]{1,0,2:T(2,128)(2,1)}, u32[]{:S(2)}, u32[]{:S(2)}) async-start(bf16[2,128,3072]{1,0,2:T(2,128)(2,1)} %copy.70), calls=%async_computation.2 | async-start | bytes 3145728 | tf_op jit(solution)/shard_map/all_to_all | solution.py:137
  221.2 99.8 %all-gather.9.cloned.1.call-start = ((), (), s32[]{:S(2)}) async-start(), calls=%async_computation.5 | async-start | bytes 1253376 | tf_op jit(solution)/shard_map/all_gather | solution.py:135
Sparse Core Ops, SparseCore 0:
  10.1 174.5 all-gather.4
  191.8 68.2 all-gather.6
  271.9 49.0 all-gather.8
where the time goes:
time: 333 us; the launch traced here: 332 us
  waiting for transfers between devices  182 us (55%)
  starting transfers between devices  62.9 us (19%)
  local copies, waits for them, and re-layouts  30.8 us (9%)
  blocking collectives  20.3 us (6%)
  between operations  15.4 us (5%)
  matrix products  12.4 us (4%)
  other arithmetic  7.8 us (2%)
    all_gather x1, waiting for transfers between devices, side_by_side(): lax.all_gather(both, axis, axis=dim, tiled=True)  90.3 us
    all_to_all x2, starting transfers between devices, copy_for_each(): return lax.all_to_all(copies, axis, split_axis=0, concat_axis=0, tiled=True)  49 us
    all_gather x1, waiting for transfers between devices, body(): lax.all_gather(attended, ('tensor', 'sub'), axis=1, tiled=True)  45.1 us
    all_gather x1, waiting for transfers between devices, body(): shards = lax.all_gather(keys_values, 'seq', axis=0, tiled=True)  38.3 us
    all_gather x1, blocking collectives, body(): lax.all_gather(summed_rows, ('tensor', 'sub'), axis=0, tiled=True)  20.3 us
    reshape x1, local copies, waits for them, and re-layouts, joined_along(): return jnp.moveaxis(tiles, 0, dim).reshape(shape)  13.8 us
    all_to_all x1, starting transfers between devices, body(): lax.all_to_all(full_columns, ('tensor', 'sub'), split_axis=2, concat_axis...  13.5 us
    all_to_all x2, waiting for transfers between devices, copy_for_each(): return lax.all_to_all(copies, axis, split_axis=0, concat_axis=0, tiled=True)  8.32 us
  transfers between devices with their start and end apart: 6, of which 4 were waited for; matrix products, arithmetic and copies ran while one was open for 14% of the time, Pallas kernels for 0%

commit v1 on v0

--- a/solution.py
+++ b/solution.py
@@ -1,9 +1,21 @@
+import functools
 import jax
 import jax.numpy as jnp
 from jax import lax
 from jax.sharding import PartitionSpec as P
+from jax.lax import all_to_all, axis_size
 
 EPSILON = 1e-06
+
+
+def feed_streams(panel, axis_key, in_dim):
+    by_rank = []
+    for _ in range(axis_size(axis_key)):
+        by_rank.append(panel)
+    return jnp.concatenate(all_to_all(jnp.stack(by_rank), axis_key, 0, 0), axis=in_dim)
+
+
+store_counts = functools.partial(feed_streams, axis_key="seq", in_dim=0)
 
 
 def copy_for_each(x, axis):
@@ -100,7 +112,7 @@
     values = jnp.concatenate([text_v, image_v], axis=0)
     keys_values = jnp.stack([keys, values], axis=2).reshape(local_rows, heads_here * 2 * head_size)
     factor = float(head_size) ** (-0.5)
-    shards = lax.all_gather(keys_values, "seq", axis=0, tiled=True)
+    shards = store_counts(keys_values)
     count = shards.shape[0]
     blocks = shards.reshape(count, heads_here, 2, head_size)
     position = jnp.arange(count, dtype=jnp.int32)

time: 333 us -> 382 us (1.15)
  waiting for transfers between devices: 182 us -> 231 us
    all_to_all x0 -> x1, waiting for transfers between devices: none -> 86.6 us  [feed_streams(): all_to_all(jnp.stack(by_rank), axis_key, 0, 0)]
    all_gather x1 -> x0, waiting for transfers between devices: 38.3 us -> none  [body(): shards = lax.all_gather(keys_values, 'seq', axis=0, tiled=True)]
    all_gather x1, waiting for transfers between devices: 45.1 us -> 17.5 us  [body(): lax.all_gather(attended, ('tensor', 'sub'), axis=1, tiled=True)]
    all_to_all x1, waiting for transfers between devices: 0.01 us -> 26.1 us  [body(): lax.all_to_all(full_columns, ('tensor', 'sub'), split_axis=2, concat_axis...]
    all_to_all x0 -> x1, starting transfers between devices: none -> 6.71 us  [feed_streams(): all_to_all(jnp.stack(by_rank), axis_key, 0, 0)]
    another operation x0 -> x3, local copies, waits for them, and re-layouts: none -> 6.4 us  [the longest x1 4.63 us: body(): blocks = shards.reshape(count, heads_here, 2, head_size)]
    all_to_all x1, starting transfers between devices: 13.5 us -> 8.06 us  [body(): lax.all_to_all(full_columns, ('tensor', 'sub'), split_axis=2, concat_axis...]
    reshape x2 -> x0, local copies, waits for them, and re-layouts: 5.4 us -> none  [the longest x1 4.63 us: body(): blocks = shards.reshape(count, heads_here, 2, head_size)]
  transfers between devices with their start and end apart: 6 -> 6, of which waited for: 4 -> 5; matrix products, arithmetic and copies ran while one was open for 14% -> 11% of each run, Pallas kernels for 0% -> 0%
where the time goes in v1:
time: 382 us
  waiting for transfers between devices  231 us (60%)
  starting transfers between devices  64.1 us (17%)
  local copies, waits for them, and re-layouts  31.8 us (8%)
  blocking collectives  20.3 us (5%)
  between operations  15.7 us (4%)
  matrix products  12.4 us (3%)
  other arithmetic  6.69 us (2%)
    all_gather x1, waiting for transfers between devices, side_by_side(): lax.all_gather(both, axis, axis=dim, tiled=True)  89.7 us
    all_to_all x1, waiting for transfers between devices, feed_streams(): all_to_all(jnp.stack(by_rank), axis_key, 0, 0)  86.6 us
    all_to_all x2, starting transfers between devices, copy_for_each(): return lax.all_to_all(copies, axis, split_axis=0, concat_axis=0, tiled=True)  49 us
    all_to_all x1, waiting for transfers between devices, body(): lax.all_to_all(full_columns, ('tensor', 'sub'), split_axis=2, concat_axis...  26.1 us
    all_gather x1, blocking collectives, body(): lax.all_gather(summed_rows, ('tensor', 'sub'), axis=0, tiled=True)  20.3 us
    all_gather x1, waiting for transfers between devices, body(): lax.all_gather(attended, ('tensor', 'sub'), axis=1, tiled=True)  17.5 us
    reshape x1, local copies, waits for them, and re-layouts, joined_along(): return jnp.moveaxis(tiles, 0, dim).reshape(shape)  13.8 us
    all_to_all x2, waiting for transfers between devices, copy_for_each(): return lax.all_to_all(copies, axis, split_axis=0, concat_axis=0, tiled=True)  10.6 us
  transfers between devices with their start and end apart: 6, of which 5 were waited for; matrix products, arithmetic and copies ran while one was open for 11% of the time, Pallas kernels for 0%

profile of v1, /device:TPU:65, one launch (start us, length us, event | category | flops | bytes accessed | tf_op | source)
XLA Modules:
  0.0 381.6 jit_solution(5290732427297364250)
XLA Ops:
  7.3 1.8 pad_maximum_fusion
  11.5 44.2 %all-to-all-start = ((f32[16,1,1152]{2,1,0:T(1,128)}), f32[16,1,1152]{2,1,0:T(1,128)S(1)}, u32[]{:S(2)}, u32[]{:S(2)}) async-start(f32[16,1,1152]{2,1,0:T(1,128)} %broadcast_in_dim.14), calls=%async_computation | async-start | bytes 147456 | tf_op jit(solution)/shard_map/all_to_all | solution.py:23
  56.6 10.6 %all-to-all-done = f32[16,1,1152]{2,1,0:T(1,128)S(1)} async-done(((f32[16,1,1152]{2,1,0:T(1,128)}), f32[16,1,1152]{2,1,0:T(1,128)S(1)}, u32[]{:S(2)}, u32[]{:S(2)}) %all-to-all-start) | async-done | bytes 73760 | tf_op jit(solution)/shard_map/all_to_all | solution.py:23
  67.3 1.5 broadcast_in_dim.22
  68.8 4.8 %all-to-all-start.2 = ((bf16[16,2,128,192]{2,3,1,0:T(8,128)(2,1)}), bf16[16,2,128,192]{2,3,1,0:T(8,128)(2,1)}, u32[]{:S(2)}, u32[]{:S(2)}) async-start(bf16[16,2,128,192]{2,3,1,0:T(8,128)(2,1)} %broadcast_in_dim.22), calls=%async_computation.2 | async-start | bytes 3145728 | tf_op jit(solution)/shard_map/all_to_all | solution.py:23
  74.9 20.3 %all-gather = f32[16,1,1152]{2,1,0:T(1,128)S(1)} all-gather(f32[1,1,1152]{2,1,0:T(1,128)S(1)} %reshape.556), channel_id=1, replica_groups=mesh['groups'=2,'seq'=16,'tensor'=8,'sub'=2] {'tensor','sub'}, dimensions={0}, use_global_device_ids=true | all-gather | bytes 78336 | tf_op jit(solution)/shard_map/all_gather | solution.py:96
  95.5 89.7 %all-gather.4.cloned.1.call-done = bf16[3072,768]{1,0:T(8,128)(2,1)} async-done(((bf16[192,768]{1,0:T(8,128)(2,1)}), bf16[3072,768]{1,0:T(8,128)(2,1)}) %all-gather.4.cloned.1.call-update) | async-done | bytes 4718608 | tf_op jit(solution)/shard_map/all_gather | solution.py:37
  185.2 2.2 fusion.14
  187.9 3.0 fusion.12
  191.5 1.6 stack.24
  193.1 6.7 %all-to-all-start.1 = ((bf16[16,288,256]{2,1,0:T(8,128)(2,1)}), bf16[16,288,256]{2,1,0:T(8,128)(2,1)S(1)}, u32[]{:S(2)}, u32[]{:S(2)}) async-start(bf16[16,288,256]{2,1,0:T(8,128)(2,1)} %stack.24), calls=%async_computation.1 | async-start | bytes 4718592 | tf_op jit(solution)/shard_map/all_to_all | solution.py:15
  200.5 1.5 copy.71
  202.0 13.8 %copy.72 = bf16[2,128,3072]{1,0,2:T(2,128)(2,1)} copy(bf16[2,128,3072]{1,2,0:T(8,128)(2,1)S(1)} %bitcast.86) | data formatting | bytes 3145728 | tf_op jit(solution)/shard_map/reshape | solution.py:43
  216.1 86.6 %all-to-all-done.1 = bf16[16,288,256]{2,1,0:T(8,128)(2,1)S(1)} async-done(((bf16[16,288,256]{2,1,0:T(8,128)(2,1)}), bf16[16,288,256]{2,1,0:T(8,128)(2,1)S(1)}, u32[]{:S(2)}, u32[]{:S(2)}) %all-to-all-start.1) | async-done | bytes 2359328 | tf_op jit(solution)/shard_map/all_to_all | solution.py:15
  302.8 8.1 %all-to-all-start.3 = ((bf16[2,128,3072]{1,0,2:T(2,128)(2,1)}), bf16[2,128,3072]{1,0,2:T(2,128)(2,1)}, u32[]{:S(2)}, u32[]{:S(2)}) async-start(bf16[2,128,3072]{1,0,2:T(2,128)(2,1)} %copy.72), calls=%async_computation.3 | async-start | bytes 3145728 | tf_op jit(solution)/shard_map/all_to_all | solution.py:149
  311.1 4.6 %reshape_reshape.3 = bf16[4608,1,2,128]{3,2,0,1:T(2,128)(2,1)S(1)} reshape(bf16[16,288,256]{2,1,0:T(8,128)(2,1)} %copy-done.1) | data formatting | bytes 4718592 | tf_op jit(solution)/shard_map/reshape;reshape | solution.py:117
  315.7 3.4 fusion.71
  319.1 1.2 fusion.74
  321.2 1.6 fusion.34
  324.1 26.1 %all-to-all-done.3 = bf16[2,128,3072]{1,0,2:T(2,128)(2,1)} async-done(((bf16[2,128,3072]{1,0,2:T(2,128)(2,1)}), bf16[2,128,3072]{1,0,2:T(2,128)(2,1)}, u32[]{:S(2)}, u32[]{:S(2)}) %all-to-all-start.3) | async-done | bytes 1572896 | tf_op jit(solution)/shard_map/all_to_all | solution.py:149
  350.2 1.6 copy.73
  353.0 17.5 %all-gather.6.cloned.1.call-done = bf16[288,2048]{1,0:T(8,128)(2,1)} async-done(((bf16[288,128]{1,0:T(8,128)(2,1)}), bf16[288,2048]{1,0:T(8,128)(2,1)}) %all-gather.6.cloned.1.call-update) | async-done | bytes 1179664 | tf_op jit(solution)/shard_map/all_gather | solution.py:147
  370.5 1.9 fusion.28
  372.4 2.4 fusion.26
  (65 shorter events, 9.3 us)
Async XLA Ops:
  7.2 3.5 copy-start
  7.2 178.0 %all-gather.4.cloned.1.call-start = ((), (), s32[]{:S(2)}) async-start(), calls=%async_computation.4 | async-start | bytes 5013504 | tf_op jit(solution)/shard_map/all_gather | solution.py:37
  11.5 55.7 %all-to-all-start = ((f32[16,1,1152]{2,1,0:T(1,128)}), f32[16,1,1152]{2,1,0:T(1,128)S(1)}, u32[]{:S(2)}, u32[]{:S(2)}) async-start(f32[16,1,1152]{2,1,0:T(1,128)} %broadcast_in_dim.14), calls=%async_computation | async-start | bytes 147456 | tf_op jit(solution)/shard_map/all_to_all | solution.py:23
  56.6 17.0 %copy-start.3 = (bf16[32,3072]{1,0:T(8,128)(2,1)S(1)}, bf16[32,3072]{1,0:T(8,128)(2,1)}, u32[]{:S(2)}) copy-start(bf16[32,3072]{1,0:T(8,128)(2,1)} %param.12) | copy-start | bytes 589828
  56.6 17.4 %copy-start.2 = (bf16[256,3072]{1,0:T(8,128)(2,1)S(1)}, bf16[256,3072]{1,0:T(8,128)(2,1)}, u32[]{:S(2)}) copy-start(bf16[256,3072]{1,0:T(8,128)(2,1)} %param.11) | copy-start | bytes 4718596
  68.8 122.7 %all-to-all-start.2 = ((bf16[16,2,128,192]{2,3,1,0:T(8,128)(2,1)}), bf16[16,2,128,192]{2,3,1,0:T(8,128)(2,1)}, u32[]{:S(2)}, u32[]{:S(2)}) async-start(bf16[16,2,128,192]{2,3,1,0:T(8,128)(2,1)} %broadcast_in_dim.22), calls=%async_computation.2 | async-start | bytes 3145728 | tf_op jit(solution)/shard_map/all_to_all | solution.py:23
  73.6 1.3 copy-start.4
  193.1 109.7 %all-to-all-start.1 = ((bf16[16,288,256]{2,1,0:T(8,128)(2,1)}), bf16[16,288,256]{2,1,0:T(8,128)(2,1)S(1)}, u32[]{:S(2)}, u32[]{:S(2)}) async-start(bf16[16,288,256]{2,1,0:T(8,128)(2,1)} %stack.24), calls=%async_computation.1 | async-start | bytes 4718592 | tf_op jit(solution)/shard_map/all_to_all | solution.py:15
  302.8 8.1 %copy-start.1 = (bf16[16,288,256]{2,1,0:T(8,128)(2,1)}, bf16[16,288,256]{2,1,0:T(8,128)(2,1)S(1)}, u32[]{:S(2)}) copy-start(bf16[16,288,256]{2,1,0:T(8,128)(2,1)S(1)} %all-to-all-done.1) | copy-start | bytes 7077892
  302.8 47.5 %all-to-all-start.3 = ((bf16[2,128,3072]{1,0,2:T(2,128)(2,1)}), bf16[2,128,3072]{1,0,2:T(2,128)(2,1)}, u32[]{:S(2)}, u32[]{:S(2)}) async-start(bf16[2,128,3072]{1,0,2:T(2,128)(2,1)} %copy.72), calls=%async_computation.3 | async-start | bytes 3145728 | tf_op jit(solution)/shard_map/all_to_all | solution.py:149
  310.8 59.7 %all-gather.6.cloned.1.call-start = ((), (), s32[]{:S(2)}) async-start(), calls=%async_computation.5 | async-start | bytes 1253376 | tf_op jit(solution)/shard_map/all_gather | solution.py:147
Sparse Core Ops, SparseCore 0:
  10.1 175.0 all-gather.3
  323.0 47.4 all-gather.5
